TPU v7x, 32 devices: a whole 2x2x4 slice. The times are simulated.
32 devices in a mesh: patch: 16 (over z, y, x), batch: 2 (over core).
Axes of the slice: x: 2, y: 2, z: 4, core: 2. Of those that a mesh axis runs over, the one named last changes fastest.
Arguments:
- tokens: bfloat16 [4096, 1152], P(('batch', 'patch')), parts along dimension 0, may hold values from -6 to 6
- slots: int32 [4096], P(('batch', 'patch')), parts along dimension 0, may hold values from 0 to 127, as said below
- counts: int32 [32], P(('batch', 'patch')), parts along dimension 0, may hold values from 32 to 128, as said below
- shift: float32 [1152], replicated, may hold values from -3 to 3
- scale: float32 [1152], replicated, may hold values from -3 to 3
- gate: float32 [1152], replicated, may hold values from -4 to 4
- w_qkv: bfloat16 [1152, 3456], replicated, may hold values from -1 to 1
- w_out: bfloat16 [1152, 1152], replicated, may hold values from -0.1875 to 0.1875
Outputs:
- result: bfloat16 [4096, 1152], P(('batch', 'patch')), parts along dimension 0
There are 2 independent parts, one for each index of `batch`. A program takes and returns all parts, laid end to end along the dimension named above; an argument that names none is the same for every part. Nothing has to cross between parts.
Inputs may be any that keep to these rules, and one draw needn't show every extreme that they name: `counts`: at least a quarter of each block's slots are live. The live slots of all blocks of an image number exactly 80 times the number of patch devices, and all blocks of some device are full. `slots`: every token's slot is below its block's count, and every slot below the count holds at least one token.
All inputs are finite; a program needn't handle non-finite values.
Results may differ from a plain program's by a relative error of at most 0.011.
Values may be sent and summed in bfloat16 or wider, within the bound.
A program may use at most 192 MiB of HBM per device.

v0:
```python
import jax
import jax.numpy as jnp
from jax import lax
from jax.sharding import PartitionSpec as P

HEADS = 16
BLK = 128


def layer_norm(merged, shift, scale):
    values = merged.astype(jnp.float32)
    center = jnp.mean(values, axis=-1, keepdims=True)
    spread = jnp.mean((values - center) ** 2, axis=-1, keepdims=True)
    return ((values - center) * lax.rsqrt(spread + 1e-06) * (1.0 + scale) + shift).astype(
        jnp.bfloat16
    )


def size_bias(sizes):
    return jnp.log(jnp.maximum(sizes.astype(jnp.float32), 1.0))


def empty_carry(heads, query_rows, head_size):
    return (
        jnp.full((heads, query_rows), -1e30, jnp.float32),
        jnp.zeros((heads, query_rows), jnp.float32),
        jnp.zeros((heads, query_rows, head_size), jnp.float32),
    )


def finish(accum, total):
    heads, query_rows, head_size = accum.shape
    return (
        (accum / total[:, :, None])
        .transpose(1, 0, 2)
        .reshape(query_rows, heads * head_size)
        .astype(jnp.bfloat16)
    )


def attend_piece(query, carry, keys, values, bias, inverse):
    top, total, accum = carry
    key_rows = keys.shape[0]
    heads = query.shape[1]
    key_heads = keys.reshape(key_rows, heads, -1)
    value_heads = values.reshape(key_rows, heads, -1)
    score = (
        jnp.einsum("qhe,khe->hqk", query, key_heads, preferred_element_type=jnp.float32) * inverse
        + bias[None, None, :]
    )
    new_top = jnp.maximum(top, jnp.max(score, axis=-1))
    probs = jnp.exp(score - new_top[:, :, None])
    total = jnp.sum(probs, axis=-1)
    update = jnp.einsum(
        "hqk,khe->hqe", probs.astype(jnp.bfloat16), value_heads, preferred_element_type=jnp.float32
    )
    return (new_top, total, update)


def body(tokens, slots, counts, shift, scale, gate, w_qkv, w_out):
    rows, width = tokens.shape
    nblk = rows // BLK
    heads = HEADS
    head_size = width // heads
    inverse = 1.0 / head_size**0.5
    onehot = slots.reshape(nblk, BLK)[:, :, None] == jnp.arange(BLK, dtype=jnp.int32)[None, None, :]
    sums = jnp.einsum(
        "bts,btd->bsd",
        onehot.astype(jnp.bfloat16),
        tokens.reshape(nblk, BLK, width),
        preferred_element_type=jnp.float32,
    )
    members = jnp.sum(onehot.astype(jnp.float32), axis=1)
    merged = (
        (sums / jnp.maximum(members, 1.0)[:, :, None]).astype(jnp.bfloat16).reshape(rows, width)
    )
    normed = layer_norm(merged, shift, scale)
    sizes = members.reshape(rows).astype(jnp.bfloat16)
    qkv = jnp.dot(normed, w_qkv, preferred_element_type=jnp.float32)
    query = qkv[:, :width].astype(jnp.bfloat16)
    keys = qkv[:, width : 2 * width].astype(jnp.bfloat16)
    values = qkv[:, 2 * width :].astype(jnp.bfloat16)
    alive = (
        (jnp.arange(BLK, dtype=jnp.int32)[None, :] < counts[:, None])
        .reshape(rows)
        .astype(jnp.bfloat16)
    )
    query_heads = query.reshape(rows, heads, head_size)
    keys_part = lax.all_gather(keys, "patch", axis=0, tiled=True)
    values_part = lax.all_gather(values, "patch", axis=0, tiled=True)
    sizes_part = lax.all_gather(sizes, "patch", axis=0, tiled=True)
    alive_part = lax.all_gather(alive, "patch", axis=0, tiled=True)
    bias = jnp.where(alive_part > 0, size_bias(sizes_part), -1e30)
    top, total, accum = attend_piece(
        query_heads, empty_carry(heads, rows, head_size), keys_part, values_part, bias, inverse
    )
    attended = finish(accum, total)
    projected = jnp.dot(attended, w_out, preferred_element_type=jnp.float32)
    branch = jnp.einsum(
        "bts,bsd->btd",
        onehot.astype(jnp.float32),
        projected.reshape(nblk, BLK, width),
        precision=lax.Precision.HIGHEST,
    ).reshape(rows, width)
    return (tokens.astype(jnp.float32) + gate * branch).astype(jnp.bfloat16)


def solution(mesh):
    return jax.shard_map(
        body,
        mesh=mesh,
        in_specs=(
            P(("batch", "patch"), None),
            P(("batch", "patch")),
            P(("batch", "patch")),
            P(),
            P(),
            P(),
            P(),
            P(),
        ),
        out_specs=P(("batch", "patch"), None),
        check_vma=False,
    )
```

profile of v0, /device:TPU:0, one launch (start us, length us, event | category | flops | bytes accessed | tf_op | source)
XLA Modules:
  0.0 205.7 jit_solution(10820672473933980348)
XLA Ops:
  6.5 0.0 copy-start
  6.5 0.0 all-gather.5.cloned.1.call-start
  6.5 0.9 convert_reduce_fusion
  7.5 1.4 fusion.27
  8.9 0.2 multiply_reduce_fusion
  9.1 0.7 broadcast_add_fusion
  9.8 4.7 %convolution_convert_fusion = bf16[128,3456]{1,0:T(8,128)(2,1)S(1)} fusion(bf16[1152,3456]{1,0:T(8,128)(2,1)} %param.14, f32[128,1152]{1,0:T(8,128)S(1)} %get-tuple-element.11, f32[1152]{0:T(1024)} %param.11, f32[1152]{0:T(1024)S(1)} %broadcast_add_fusion, f32[128]{0:T(128)S(1)} %add_rsqrt_fusion, f32[128]{0:T(128)S(1)} %broadcast_multiply_fusion), kind=kOutput, calls=%fused_computation.6 | convolution fusion | flops 1020395520 | bytes 9447424 | tf_op jit(solution)/shard_map/dot_general | solution.py:79
  14.5 0.9 fusion.26
  15.4 0.0 all-gather.5.cloned.1.call-update
  15.4 0.0 all-gather.7.cloned.1.call-start
  15.5 0.7 all-gather.7.cloned.1.call-update
  16.2 0.2 copy.18
  17.1 42.7 %all-gather.1 = bf16[16,1,128]{2,1,0:T(2,128)(2,1)S(1)} all-gather(bf16[1,1,128]{2,1,0:T(2,128)(2,1)S(1)} %get-tuple-element.8), channel_id=1, replica_groups=mesh['patch'=16,'batch'=2] {'patch'}, dimensions={0}, use_global_device_ids=true | all-gather | bytes 4352 | tf_op jit(solution)/shard_map/all_gather | solution.py:91
  59.7 36.4 %all-gather = bf16[16,1,128]{2,1,0:T(2,128)(2,1)S(1)} all-gather(bf16[1,1,128]{2,1,0:T(2,128)(2,1)S(1)} %fusion.24), channel_id=1, replica_groups=mesh['patch'=16,'batch'=2] {'patch'}, dimensions={0}, use_global_device_ids=true | all-gather | bytes 4352 | tf_op jit(solution)/shard_map/all_gather | solution.py:92
  96.1 2.0 all-gather.5.cloned.1.call-done
  98.1 6.7 %copy.19 = bf16[2048,1152]{0,1:T(8,128)(2,1)} copy(bf16[2048,1152]{1,0:T(8,128)(2,1)} %all-gather.5.cloned.1.call-done) | data formatting | bytes 9437184 | tf_op jit(solution)/shard_map/all_gather | solution.py:89
  104.9 4.5 %fusion = (f32[16,128]{1,0:T(8,128)S(1)}, f32[16,128,2048]{2,1,0:T(8,128)S(1)}) fusion(f32[2048]{0:T(1024)S(1)} %bitcast.30, bf16[128,16,72]{0,2,1:T(8,128)(2,1)S(1)} %bitcast.28, bf16[2048,16,72]{0,2,1:T(8,128)(2,1)} %bitcast.26), kind=kOutput, calls=%fused_computation.2 | convolution fusion | flops 616560640 | bytes 21807104 | tf_op jit(solution)/shard_map/qhe,khe->hqk/dot_general | solution.py:48
  109.3 0.0 copy-start.1
  109.4 5.7 %copy-done.1 = f32[16,128,2048]{2,1,0:T(8,128)} copy-done((f32[16,128,2048]{2,1,0:T(8,128)}, f32[16,128,2048]{2,1,0:T(8,128)S(1)}, u32[]{:S(2)}) %copy-start.1) | copy-done | bytes 16777240
  115.1 3.8 %fusion.1 = f32[16,128]{1,0:T(8,128)S(1)} fusion(f32[16,128,2048]{2,1,0:T(8,128)S(1)} %get-tuple-element.13, f32[16,128]{1,0:T(8,128)S(1)} %broadcast_maximum_fusion, f32[2048]{0:T(1024)S(1)} %bitcast.31), kind=kLoop, calls=%fused_computation.3 | loop fusion | flops 16775168 | bytes 16801792 | tf_op jit(solution)/shard_map/reduce_sum | solution.py:53
  118.8 60.6 %all-gather.7.cloned.1.call-done = bf16[2048,1152]{1,0:T(8,128)(2,1)} async-done(((bf16[128,1152]{1,0:T(8,128)(2,1)}), bf16[2048,1152]{1,0:T(8,128)(2,1)}) %all-gather.7.cloned.1.call-update) | async-done | bytes 4718608 | tf_op jit(solution)/shard_map/all_gather | solution.py:90
  179.4 6.7 %copy.20 = bf16[2048,1152]{0,1:T(8,128)(2,1)} copy(bf16[2048,1152]{1,0:T(8,128)(2,1)} %all-gather.7.cloned.1.call-done) | data formatting | bytes 9437184 | tf_op jit(solution)/shard_map/all_gather | solution.py:90
  186.1 0.0 copy-start.2
  186.1 0.0 copy-start.3
  186.1 0.0 copy-start.4
  186.1 10.9 %fusion.15 = bf16[128,16,72]{0,2,1:T(8,128)(2,1)S(1)} fusion(bf16[2048,16,72]{0,2,1:T(8,128)(2,1)} %bitcast.27, f32[16,128,2048]{2,1,0:T(8,128)} %copy-done.1, f32[16,128]{1,0:T(8,128)S(1)} %broadcast_maximum_fusion, f32[2048]{0:T(1024)S(1)} %bitcast.32, f32[128,16]{0,1:T(8,128)S(1)} %bitcast.33), kind=kOutput, calls=%fused_computation.15 | convolution fusion | flops 621051904 | bytes 21815296 | tf_op jit(solution)/shard_map/hqk,khe->hqe/dot_general | solution.py:54
  197.0 0.0 copy-done
  197.0 0.6 fusion.28
  197.6 0.0 copy-done.2
  197.6 0.0 copy-done.3
  197.7 0.0 copy-done.4
  197.7 1.2 fusion.8
  (6 shorter events, 0.1 us)
Async XLA Ops:
  6.5 190.5 %copy-start = (bf16[1152,1152]{1,0:T(8,128)(2,1)S(1)}, bf16[1152,1152]{1,0:T(8,128)(2,1)}, u32[]{:S(2)}) copy-start(bf16[1152,1152]{1,0:T(8,128)(2,1)} %param.15) | copy-start | bytes 7962628
  6.5 91.6 %all-gather.5.cloned.1.call-start = ((), (), s32[]{:S(2)}) async-start(), calls=%async_computation | async-start | bytes 5013504 | tf_op jit(solution)/shard_map/all_gather | solution.py:89
  15.4 163.9 %all-gather.7.cloned.1.call-start = ((), (), s32[]{:S(2)}) async-start(), calls=%async_computation.1 | async-start | bytes 5013504 | tf_op jit(solution)/shard_map/all_gather | solution.py:90
  109.3 5.7 %copy-start.1 = (f32[16,128,2048]{2,1,0:T(8,128)}, f32[16,128,2048]{2,1,0:T(8,128)S(1)}, u32[]{:S(2)}) copy-start(f32[16,128,2048]{2,1,0:T(8,128)S(1)} %get-tuple-element.13) | copy-start | bytes 50331652
  186.1 11.5 %copy-start.2 = (bf16[128,1152]{1,0:T(8,128)(2,1)S(1)}, bf16[128,1152]{1,0:T(8,128)(2,1)}, u32[]{:S(2)}) copy-start(bf16[128,1152]{1,0:T(8,128)(2,1)} %param.8) | copy-start | bytes 884740
  186.1 11.5 %copy-start.3 = (f32[1152]{0:T(1024)S(1)}, f32[1152]{0:T(1024)}, u32[]{:S(2)}) copy-start(f32[1152]{0:T(1024)} %param.13) | copy-start | bytes 13828
  186.1 11.5 %copy-start.4 = (s32[128]{0:T(128)S(1)}, s32[128]{0:T(128)}, u32[]{:S(2)}) copy-start(s32[128]{0:T(128)} %param.9) | copy-start | bytes 1540
Sparse Core Ops, SparseCore 0:
  15.6 82.5 all-gather.4
  100.9 78.4 all-gather.6
where the time goes:
time: 206 us
  blocking collectives  79 us (38%)
  waiting for transfers between devices  63.3 us (31%)
  matrix products  23.3 us (11%)
  local copies, waits for them, and re-layouts  20.3 us (10%)
  between operations  14.2 us (7%)
  other arithmetic  5.63 us (3%)
    all_gather x1, waiting for transfers between devices, body(): values_part = lax.all_gather(values, 'patch', axis=0, tiled=True)  60.6 us
    all_gather x1, blocking collectives, body(): sizes_part = lax.all_gather(sizes, 'patch', axis=0, tiled=True)  42.7 us
    all_gather x1, blocking collectives, body(): alive_part = lax.all_gather(alive, 'patch', axis=0, tiled=True)  36.4 us
    dot_general x1, matrix products, attend_piece(): jnp.einsum('hqk,khe->hqe', probs.astype(jnp.bfloat16), value_heads, prefe...  10.9 us
    all_gather x1, local copies, waits for them, and re-layouts, body(): values_part = lax.all_gather(values, 'patch', axis=0, tiled=True)  6.74 us
    all_gather x1, local copies, waits for them, and re-layouts, body(): keys_part = lax.all_gather(keys, 'patch', axis=0, tiled=True)  6.74 us
    unnamed x10, local copies, waits for them, and re-layouts  5.71 us
    dot_general x1, matrix products, body(): qkv = jnp.dot(normed, w_qkv, preferred_element_type=jnp.float32)  4.71 us
  transfers between devices with their start and end apart: 2, of which 2 were waited for; matrix products, arithmetic and copies ran while one was open for 7% of the time, Pallas kernels for 0%

commit v1 on v0

--- a/solution.py
+++ b/solution.py
@@ -89,7 +89,10 @@
     keys_part = lax.all_gather(keys, "patch", axis=0, tiled=True)
     values_part = lax.all_gather(values, "patch", axis=0, tiled=True)
     sizes_part = lax.all_gather(sizes, "patch", axis=0, tiled=True)
-    alive_part = lax.all_gather(alive, "patch", axis=0, tiled=True)
+    frame_out = lax.axis_size("patch")
+    y_new = jnp.stack(frame_out * [alive], axis=0)
+    back = lax.all_to_all(y_new, "patch", 0, 0)
+    alive_part = jnp.concatenate(back, 0)
     bias = jnp.where(alive_part > 0, size_bias(sizes_part), -1e30)
     top, total, accum = attend_piece(
         query_heads, empty_carry(heads, rows, head_size), keys_part, values_part, bias, inverse

time: 206 us -> 206 us (level)
  blocking collectives: 79 us -> 41.2 us
  waiting for transfers between devices: 63.3 us -> 92.1 us
  starting transfers between devices: 0.04 us -> 8.38 us
    all_gather x1 -> x0, blocking collectives: 36.4 us -> none  [body(): alive_part = lax.all_gather(alive, 'patch', axis=0, tiled=True)]
    all_gather x1, waiting for transfers between devices: 1.98 us -> 30.8 us  [body(): keys_part = lax.all_gather(keys, 'patch', axis=0, tiled=True)]
    all_to_all x0 -> x1, starting transfers between devices: none -> 8.34 us  [body(): back = lax.all_to_all(y_new, 'patch', 0, 0)]
  transfers between devices with their start and end apart: 2 -> 3, of which waited for: 2 -> 2; matrix products, arithmetic and copies ran while one was open for 7% -> 8% of each run, Pallas kernels for 0% -> 0%
where the time goes in v1:
time: 206 us
  waiting for transfers between devices  92.1 us (45%)
  blocking collectives  41.2 us (20%)
  matrix products  23.3 us (11%)
  local copies, waits for them, and re-layouts  20.9 us (10%)
  between operations  14.2 us (7%)
  starting transfers between devices  8.38 us (4%)
  other arithmetic  5.63 us (3%)
    all_gather x1, waiting for transfers between devices, body(): values_part = lax.all_gather(values, 'patch', axis=0, tiled=True)  60.5 us
    all_gather x1, blocking collectives, body(): sizes_part = lax.all_gather(sizes, 'patch', axis=0, tiled=True)  41.2 us
    all_gather x1, waiting for transfers between devices, body(): keys_part = lax.all_gather(keys, 'patch', axis=0, tiled=True)  30.8 us
    dot_general x1, matrix products, attend_piece(): jnp.einsum('hqk,khe->hqe', probs.astype(jnp.bfloat16), value_heads, prefe...  10.9 us
    all_to_all x1, starting transfers between devices, body(): back = lax.all_to_all(y_new, 'patch', 0, 0)  8.34 us
    all_gather x1, local copies, waits for them, and re-layouts, body(): keys_part = lax.all_gather(keys, 'patch', axis=0, tiled=True)  6.73 us
    all_gather x1, local copies, waits for them, and re-layouts, body(): values_part = lax.all_gather(values, 'patch', axis=0, tiled=True)  6.72 us
    unnamed x10, local copies, waits for them, and re-layouts  5.73 us
  transfers between devices with their start and end apart: 3, of which 2 were waited for; matrix products, arithmetic and copies ran while one was open for 8% of the time, Pallas kernels for 0%

profile of v1, /device:TPU:0, one launch (start us, length us, event | category | flops | bytes accessed | tf_op | source)
XLA Modules:
  0.0 205.6 jit_solution(15018438547929240242)
XLA Ops:
  6.5 0.0 copy-start
  6.5 0.0 all-gather.4.cloned.1.call-start
  6.5 0.9 convert_reduce_fusion
  7.5 1.4 fusion.26
  8.9 0.2 multiply_reduce_fusion
  9.1 0.7 broadcast_add_fusion
  9.8 4.7 %convolution_convert_fusion = bf16[128,3456]{1,0:T(8,128)(2,1)S(1)} fusion(bf16[1152,3456]{1,0:T(8,128)(2,1)} %param.14, f32[128,1152]{1,0:T(8,128)S(1)} %get-tuple-element.11, f32[1152]{0:T(1024)} %param.11, f32[1152]{0:T(1024)S(1)} %broadcast_add_fusion, f32[128]{0:T(128)S(1)} %add_rsqrt_fusion, f32[128]{0:T(128)S(1)} %broadcast_multiply_fusion), kind=kOutput, calls=%fused_computation.6 | convolution fusion | flops 1020395520 | bytes 9447424 | tf_op jit(solution)/shard_map/dot_general | solution.py:79
  14.5 0.9 fusion.25
  15.4 0.0 all-gather.4.cloned.1.call-update
  15.5 0.0 all-gather.6.cloned.1.call-start
  15.5 0.7 all-gather.6.cloned.1.call-update
  16.9 0.6 stack.2
  17.5 8.3 %all-to-all-start = ((bf16[16,1,128]{2,1,0:T(2,128)(2,1)}), bf16[16,1,128]{2,1,0:T(2,128)(2,1)S(1)}, u32[]{:S(2)}, u32[]{:S(2)}) async-start(bf16[16,1,128]{2,1,0:T(2,128)(2,1)} %stack.2), calls=%async_computation | async-start | bytes 16384 | tf_op jit(solution)/shard_map/all_to_all | solution.py:94
  25.8 0.2 copy.18
  26.0 41.2 %all-gather = bf16[16,1,128]{2,1,0:T(2,128)(2,1)S(1)} all-gather(bf16[1,1,128]{2,1,0:T(2,128)(2,1)S(1)} %get-tuple-element.8), channel_id=1, replica_groups=mesh['patch'=16,'batch'=2] {'patch'}, dimensions={0}, use_global_device_ids=true | all-gather | bytes 4352 | tf_op jit(solution)/shard_map/all_gather | solution.py:91
  67.2 0.0 all-to-all-done
  67.3 30.8 %all-gather.4.cloned.1.call-done = bf16[2048,1152]{1,0:T(8,128)(2,1)} async-done(((bf16[128,1152]{1,0:T(8,128)(2,1)}), bf16[2048,1152]{1,0:T(8,128)(2,1)}) %all-gather.4.cloned.1.call-update) | async-done | bytes 4718608 | tf_op jit(solution)/shard_map/all_gather | solution.py:89
  98.1 6.7 %copy.19 = bf16[2048,1152]{0,1:T(8,128)(2,1)} copy(bf16[2048,1152]{1,0:T(8,128)(2,1)} %all-gather.4.cloned.1.call-done) | data formatting | bytes 9437184 | tf_op jit(solution)/shard_map/all_gather | solution.py:89
  104.8 4.5 %fusion = (f32[16,128]{1,0:T(8,128)S(1)}, f32[16,128,2048]{2,1,0:T(8,128)S(1)}) fusion(f32[2048]{0:T(1024)S(1)} %bitcast.28, bf16[128,16,72]{0,2,1:T(8,128)(2,1)S(1)} %bitcast.26, bf16[2048,16,72]{0,2,1:T(8,128)(2,1)} %bitcast.24), kind=kOutput, calls=%fused_computation.2 | convolution fusion | flops 616560640 | bytes 21807104 | tf_op jit(solution)/shard_map/qhe,khe->hqk/dot_general | solution.py:48
  109.3 0.0 copy-start.1
  109.3 5.7 %copy-done.1 = f32[16,128,2048]{2,1,0:T(8,128)} copy-done((f32[16,128,2048]{2,1,0:T(8,128)}, f32[16,128,2048]{2,1,0:T(8,128)S(1)}, u32[]{:S(2)}) %copy-start.1) | copy-done | bytes 16777240
  115.0 3.8 %fusion.1 = f32[16,128]{1,0:T(8,128)S(1)} fusion(f32[16,128,2048]{2,1,0:T(8,128)S(1)} %get-tuple-element.13, f32[16,128]{1,0:T(8,128)S(1)} %broadcast_maximum_fusion, f32[2048]{0:T(1024)S(1)} %bitcast.29), kind=kLoop, calls=%fused_computation.3 | loop fusion | flops 16775168 | bytes 16801792 | tf_op jit(solution)/shard_map/reduce_sum | solution.py:53
  118.8 60.5 %all-gather.6.cloned.1.call-done = bf16[2048,1152]{1,0:T(8,128)(2,1)} async-done(((bf16[128,1152]{1,0:T(8,128)(2,1)}), bf16[2048,1152]{1,0:T(8,128)(2,1)}) %all-gather.6.cloned.1.call-update) | async-done | bytes 4718608 | tf_op jit(solution)/shard_map/all_gather | solution.py:90
  179.4 6.7 %copy.20 = bf16[2048,1152]{0,1:T(8,128)(2,1)} copy(bf16[2048,1152]{1,0:T(8,128)(2,1)} %all-gather.6.cloned.1.call-done) | data formatting | bytes 9437184 | tf_op jit(solution)/shard_map/all_gather | solution.py:90
  186.1 0.0 copy-start.2
  186.1 10.9 %fusion.15 = bf16[128,16,72]{0,2,1:T(8,128)(2,1)S(1)} fusion(bf16[2048,16,72]{0,2,1:T(8,128)(2,1)} %bitcast.25, f32[16,128,2048]{2,1,0:T(8,128)} %copy-done.1, f32[16,128]{1,0:T(8,128)S(1)} %broadcast_maximum_fusion, f32[2048]{0:T(1024)S(1)} %bitcast.30, f32[128,16]{0,1:T(8,128)S(1)} %bitcast.31), kind=kOutput, calls=%fused_computation.15 | convolution fusion | flops 621051904 | bytes 21815296 | tf_op jit(solution)/shard_map/hqk,khe->hqe/dot_general | solution.py:54
  196.9 0.0 copy-done
  197.0 0.6 fusion.27
  197.6 0.0 copy-done.2
  197.6 0.0 copy-done.3
  197.6 0.0 copy-done.4
  197.6 1.2 fusion.8
  (8 shorter events, 0.1 us)
Async XLA Ops:
  6.5 190.4 %copy-start = (bf16[1152,1152]{1,0:T(8,128)(2,1)S(1)}, bf16[1152,1152]{1,0:T(8,128)(2,1)}, u32[]{:S(2)}) copy-start(bf16[1152,1152]{1,0:T(8,128)(2,1)} %param.15) | copy-start | bytes 7962628
  6.5 91.6 %all-gather.4.cloned.1.call-start = ((), (), s32[]{:S(2)}) async-start(), calls=%async_computation.1 | async-start | bytes 5013504 | tf_op jit(solution)/shard_map/all_gather | solution.py:89
  15.5 163.9 %all-gather.6.cloned.1.call-start = ((), (), s32[]{:S(2)}) async-start(), calls=%async_computation.2 | async-start | bytes 5013504 | tf_op jit(solution)/shard_map/all_gather | solution.py:90
  17.5 49.8 %all-to-all-start = ((bf16[16,1,128]{2,1,0:T(2,128)(2,1)}), bf16[16,1,128]{2,1,0:T(2,128)(2,1)S(1)}, u32[]{:S(2)}, u32[]{:S(2)}) async-start(bf16[16,1,128]{2,1,0:T(2,128)(2,1)} %stack.2), calls=%async_computation | async-start | bytes 16384 | tf_op jit(solution)/shard_map/all_to_all | solution.py:94
  109.3 5.7 %copy-start.1 = (f32[16,128,2048]{2,1,0:T(8,128)}, f32[16,128,2048]{2,1,0:T(8,128)S(1)}, u32[]{:S(2)}) copy-start(f32[16,128,2048]{2,1,0:T(8,128)S(1)} %get-tuple-element.13) | copy-start | bytes 50331652
  186.1 11.5 %copy-start.2 = (bf16[128,1152]{1,0:T(8,128)(2,1)S(1)}, bf16[128,1152]{1,0:T(8,128)(2,1)}, u32[]{:S(2)}) copy-start(bf16[128,1152]{1,0:T(8,128)(2,1)} %param.8) | copy-start | bytes 884740
  186.1 11.5 %copy-start.3 = (f32[1152]{0:T(1024)S(1)}, f32[1152]{0:T(1024)}, u32[]{:S(2)}) copy-start(f32[1152]{0:T(1024)} %param.13) | copy-start | bytes 13828
  186.1 11.5 %copy-start.4 = (s32[128]{0:T(128)S(1)}, s32[128]{0:T(128)}, u32[]{:S(2)}) copy-start(s32[128]{0:T(128)} %param.9) | copy-start | bytes 1540
Sparse Core Ops, SparseCore 0:
  15.6 82.4 all-gather.3
  100.9 78.4 all-gather.5
